TPU v7x, 128 devices: a whole 4x4x4 slice. The times are simulated.
128 devices in a mesh: dp: 32 (over y, z, core), fsdp: 4 (over x).
Axes of the slice: x: 4, y: 4, z: 4, core: 2. Of those that a mesh axis runs over, the one named last changes fastest.
Arguments:
- tokens: bfloat16 [65536, 4096], P(('dp', 'fsdp')), may hold values from -0.75 to 0.75
- doc_ids: int32 [65536], P(('dp', 'fsdp')), may hold values from 0 to 63, never falling along the last dimension, each value on 1 to 2048 neighbouring positions
- attn_gain: float32 [4096], replicated, may hold values from 0.1 to 1.9
- mlp_gain: float32 [4096], replicated, may hold values from 0.1 to 1.9
- w_query: bfloat16 [4096, 512], P(('dp', 'fsdp')), may hold values from -1 to 1
- w_key_value: bfloat16 [4096, 256], P(('dp', 'fsdp')), may hold values from -3 to 3
- w_out: bfloat16 [512, 4096], P(None, ('dp', 'fsdp')), may hold values from -0.25 to 0.25
- w_gate: bfloat16 [4096, 1024], P(('dp', 'fsdp')), may hold values from -0.09375 to 0.09375
- w_up: bfloat16 [4096, 1024], P(('dp', 'fsdp')), may hold values from -0.09375 to 0.09375
- w_down: bfloat16 [1024, 4096], P(None, ('dp', 'fsdp')), may hold values from -0.1875 to 0.1875
Outputs:
- mixed: bfloat16 [65536, 4096], P(('dp', 'fsdp'))
Inputs may be any that keep to these rules, and one draw needn't show every extreme that they name: `doc_ids`: document numbers never fall along the pack, and every document has at most 2048 tokens.
All inputs are finite; a program needn't handle non-finite values.
Results may differ from a plain program's by a relative error of at most 0.02.
The roundings to bfloat16 on the way count: a program that leaves them out, or rounds other values in their place, can miss the bound.
Values may be sent and summed in bfloat16 or wider, within the bound.
No kernel may reach another device: no remote copies, remote signals or barrier semaphores. Data moves between devices by JAX's collectives and lax.ppermute only.
A program may use at most 128 MiB of HBM per device.

v0:
```python
import math

import jax
import jax.numpy as jnp
from jax import lax
from jax.sharding import PartitionSpec as P

SPAN = 4


EPS = 1e-05
THETA = 500000.0
NEGATIVE = -1e30


def sent_together(arrays, axis, dim, along):
    widths = [a.shape[along] for a in arrays]
    both = jnp.concatenate(arrays, axis=along)
    out = lax.all_gather(both, axis, axis=dim, tiled=True)
    return tuple(jnp.split(out, [sum(widths[:k]) for k in range(1, len(widths))], axis=along))


def shifted(array, axis, by):
    length = lax.axis_size(axis)
    pairs = [(i, i + by) for i in range(length) if 0 <= i + by < length]
    return lax.ppermute(array, axis, pairs)


def rms_scale(values, gain):
    wide = values.astype(jnp.float32)
    power = jnp.mean(wide * wide, axis=-1, keepdims=True)
    return (wide * lax.rsqrt(power + EPS) * gain).astype(jnp.bfloat16)


def rotate(values, position):
    head = values.shape[-1]
    half = head // 2
    freqs = THETA ** (-2.0 * jnp.arange(half, dtype=jnp.float32) / head)
    angle = position.astype(jnp.float32)[:, None, None] * freqs[None, None, :]
    cosine = jnp.cos(angle)
    sine = jnp.sin(angle)
    first = values[..., :half]
    second = values[..., half:]
    return jnp.concatenate(
        [first * cosine - second * sine, second * cosine + first * sine], axis=-1
    )


def head_scores(query, keys):
    return jnp.einsum("qhd,kd->hqk", query, keys, preferred_element_type=jnp.float32) / math.sqrt(
        query.shape[-1]
    )


def weigh_values(weights, values):
    return jnp.einsum(
        "hqk,kd->qhd", weights.astype(jnp.bfloat16), values, preferred_element_type=jnp.float32
    )


def attend_live(query, halo_pairs, halo_marks, own_pairs, marks, block):
    head = query.shape[-1]
    index = jnp.arange(query.shape[0], dtype=jnp.int32)
    allowed = (marks[None, :] == marks[:, None]) & (index[None, :] <= index[:, None])
    own_scores = jnp.where(allowed[None, :, :], head_scores(query, own_pairs[:, :head]), NEGATIVE)
    count = halo_marks.shape[0] // block
    live = jnp.sum(jnp.any(halo_marks.reshape(count, block) == marks[0], axis=1).astype(jnp.int32))
    peak = jnp.max(own_scores, axis=2)
    weights = jnp.exp(own_scores - peak[:, :, None])
    totals = jnp.sum(weights, axis=2)
    mixed = weigh_values(weights, own_pairs[:, head:])

    def add_block(step, carry):
        old_peak, old_totals, old_mixed = carry
        begin = (count - 1 - step) * block
        pairs = lax.dynamic_slice_in_dim(halo_pairs, begin, block, 0)
        block_marks = lax.dynamic_slice_in_dim(halo_marks, begin, block, 0)
        same = (block_marks[None, :] == marks[:, None])[None, :, :]
        scores = jnp.where(same, head_scores(query, pairs[:, :head]), NEGATIVE)
        new_peak = jnp.maximum(old_peak, jnp.max(scores, axis=2))
        factor = jnp.exp(old_peak - new_peak)
        block_weights = jnp.exp(scores - new_peak[:, :, None])
        new_totals = old_totals * factor + jnp.sum(block_weights, axis=2)
        new_mixed = old_mixed * jnp.transpose(factor)[:, :, None] + weigh_values(
            block_weights, pairs[:, head:]
        )
        return (new_peak, new_totals, new_mixed)

    peak, totals, mixed = lax.fori_loop(0, live, add_block, (peak, totals, mixed))
    return mixed / jnp.transpose(totals)[:, :, None]


def per_device(
    tokens, doc_ids, attn_gain, mlp_gain, w_query, w_key_value, w_out, w_gate, w_up, w_down
):
    rows = tokens.shape[0]
    rank = lax.axis_index(("dp", "fsdp"))
    normed = rms_scale(tokens, attn_gain)
    query_width = w_query.shape[1]
    pair_width = w_key_value.shape[1]
    head = pair_width // 2
    heads = query_width // head
    group_query, group_pair = sent_together((w_query, w_key_value), "fsdp", 0, 1)
    pieces = sent_together((group_query, group_pair), "dp", 0, 1)
    columns = normed
    query_raw = jnp.dot(columns, pieces[0], preferred_element_type=jnp.float32)
    pair_raw = jnp.dot(columns, pieces[1], preferred_element_type=jnp.float32)
    position = rank * rows + jnp.arange(rows, dtype=jnp.int32)
    query = rotate(query_raw.reshape(rows, heads, head), position).astype(jnp.bfloat16)
    keys = rotate(pair_raw[:, None, :head], position)[:, 0, :].astype(jnp.bfloat16)
    values = pair_raw[:, head:].astype(jnp.bfloat16)
    own_pairs = jnp.concatenate([keys, values], axis=1)
    marks = doc_ids + 1
    pair_pieces = []
    mark_pieces = []
    for distance in range(SPAN, 0, -1):
        moved_pairs, moved_marks = shifted((own_pairs, marks), ("dp", "fsdp"), distance)
        pair_pieces.append(moved_pairs)
        mark_pieces.append(moved_marks)
    halo_pairs = jnp.concatenate(pair_pieces, axis=0)
    halo_marks = jnp.concatenate(mark_pieces, axis=0)
    mixed = attend_live(query, halo_pairs, halo_marks, own_pairs, marks, rows)
    attended = mixed.reshape(rows, query_width).astype(jnp.bfloat16)
    projected = jnp.dot(
        attended,
        lax.all_gather(w_out, ("dp", "fsdp"), axis=1, tiled=True),
        preferred_element_type=jnp.float32,
    )
    resid = (tokens.astype(jnp.float32) + projected).astype(jnp.bfloat16)
    resid = lax.optimization_barrier(resid)
    normed_mlp = rms_scale(resid, mlp_gain)
    group_gate, group_up = sent_together((w_gate, w_up), "fsdp", 0, 1)
    pieces = sent_together((group_gate, group_up), "dp", 0, 1)
    columns = normed_mlp
    gate = jnp.dot(columns, pieces[0], preferred_element_type=jnp.float32)
    up_value = jnp.dot(columns, pieces[1], preferred_element_type=jnp.float32)
    hidden = (jax.nn.silu(gate) * up_value).astype(jnp.bfloat16)
    down = jnp.dot(
        hidden,
        lax.all_gather(w_down, ("dp", "fsdp"), axis=1, tiled=True),
        preferred_element_type=jnp.float32,
    )
    return (resid.astype(jnp.float32) + down).astype(jnp.bfloat16)


def solution(mesh):
    in_specs = (
        P(("dp", "fsdp"), None),
        P(("dp", "fsdp")),
        P(),
        P(),
        P(("dp", "fsdp"), None),
        P(("dp", "fsdp"), None),
        P(None, ("dp", "fsdp")),
        P(("dp", "fsdp"), None),
        P(("dp", "fsdp"), None),
        P(None, ("dp", "fsdp")),
    )
    out_specs = P(("dp", "fsdp"), None)
    return jax.shard_map(
        per_device, mesh=mesh, in_specs=in_specs, out_specs=out_specs, check_vma=False
    )
```

profile of v0, /device:TPU:98, one launch (start us, length us, event | category | flops | bytes accessed | tf_op | source)
XLA Modules:
  0.0 302.0 jit_solution(3767838602492783908)
XLA Ops:
  6.5 0.8 pad_maximum_fusion.6
  7.3 13.0 %all_gather.18 = bf16[128,768]{1,0:T(8,128)(2,1)} all-gather(bf16[32,768]{1,0:T(8,128)(2,1)S(1)} %pad_maximum_fusion.6), channel_id=1, replica_groups=mesh['dp'=32,'fsdp'=4] {'fsdp'}, dimensions={0}, use_global_device_ids=true | all-gather | bytes 245760 | tf_op jit(solution)/shard_map/all_gather | solution.py:19
  20.4 0.7 all-gather.7.cloned.1.call-update
  21.2 0.9 pad_maximum_fusion.4
  22.1 13.5 %all_gather.21 = bf16[128,2048]{1,0:T(8,128)(2,1)} all-gather(bf16[32,2048]{1,0:T(8,128)(2,1)S(1)} %pad_maximum_fusion.4), channel_id=1, replica_groups=mesh['dp'=32,'fsdp'=4] {'fsdp'}, dimensions={0}, use_global_device_ids=true | all-gather | bytes 655360 | tf_op jit(solution)/shard_map/all_gather | solution.py:19
  35.7 0.7 broadcast_add_fusion
  36.4 1.9 collective-permute-start
  38.3 2.8 collective-permute-start.1
  41.1 3.1 %collective-permute-start.2 = (s32[512]{0:T(512)S(1)}, s32[512]{0:T(512)S(1)}, u32[]{:S(2)}, u32[]{:S(2)}) collective-permute-start(s32[512]{0:T(512)S(1)} %broadcast_add_fusion), channel_id=1, source_target_pairs={{0,2},{1,3},{2,4},{3,5},{4,6},{5,7},{6,8},{7,9},{8,10},{9,11},{10,... | collective-permute-start | bytes 6152 | tf_op jit(solution)/shard_map/ppermute | solution.py:26
  44.2 4.2 %collective-permute-start.3 = (s32[512]{0:T(512)S(1)}, s32[512]{0:T(512)S(1)}, u32[]{:S(2)}, u32[]{:S(2)}) collective-permute-start(s32[512]{0:T(512)S(1)} %broadcast_add_fusion), channel_id=1, source_target_pairs={{0,1},{1,2},{2,3},{3,4},{4,5},{5,6},{6,7},{7,8},{8,9},{9,10},{10,1... | collective-permute-start | bytes 6152 | tf_op jit(solution)/shard_map/ppermute | solution.py:26
  48.6 3.1 %fusion.17 = f32[512]{0:T(512)S(1)} fusion(bf16[512,4096]{1,0:T(8,128)(2,1)} %param.12), kind=kLoop, calls=%fused_computation.25 | loop fusion | flops 6290944 | bytes 4196352 | tf_op jit(solution)/shard_map/reduce_sum | solution.py:31
  51.7 1.0 multiply_cosine_fusion
  52.7 0.5 slice.36
  53.3 0.7 broadcast_compare_fusion.1
  54.1 0.7 convert_reduce_fusion
  54.8 14.6 %all-gather.5.cloned.1.call-done = bf16[4096,768]{1,0:T(8,128)(2,1)} async-done(((bf16[128,768]{1,0:T(8,128)(2,1)}), bf16[4096,768]{1,0:T(8,128)(2,1)}) %all-gather.5.cloned.1.call-update) | async-done | bytes 6291472 | tf_op jit(solution)/shard_map/all_gather | solution.py:19
  69.4 4.6 %fusion.34 = f32[512,256]{0,1:T(8,128)S(1)} fusion(bf16[4096,768]{1,0:T(8,128)(2,1)} %all-gather.5.cloned.1.call-done, bf16[512,4096]{1,0:T(8,128)(2,1)} %param.12, f32[4096]{0:T(1024)S(1)} %copy-done.8, f32[512]{0:T(512)S(1)} %add_rsqrt_fusion.1), kind=kOutput, calls=%fused_computation.44 | convolution fusion | flops 1082130432 | bytes 6834176 | tf_op jit(solution)/shard_map/dot_general | solution.py:107
  74.1 0.6 fusion.54
  74.6 0.7 pad_maximum_fusion.2
  75.4 2.1 collective-permute-start.4
  77.5 3.4 %collective-permute-start.5 = (bf16[512,256]{0,1:T(8,128)(2,1)}, bf16[512,256]{0,1:T(8,128)(2,1)}, u32[]{:S(2)}, u32[]{:S(2)}) collective-permute-start(bf16[512,256]{0,1:T(8,128)(2,1)} %pad_maximum_fusion.2), channel_id=1, source_target_pairs={{0,3},{1,4},{2,5},{3,6},{4,7},{5,8},{6,9},{7,10},{8,11},{9,12},{10... | collective-permute-start | bytes 786440 | tf_op jit(solution)/shard_map/ppermute | solution.py:26
  80.9 4.2 %collective-permute-start.6 = (bf16[512,256]{0,1:T(8,128)(2,1)}, bf16[512,256]{0,1:T(8,128)(2,1)}, u32[]{:S(2)}, u32[]{:S(2)}) collective-permute-start(bf16[512,256]{0,1:T(8,128)(2,1)} %pad_maximum_fusion.2), channel_id=1, source_target_pairs={{0,2},{1,3},{2,4},{3,5},{4,6},{5,7},{6,8},{7,9},{8,10},{9,11},{10,... | collective-permute-start | bytes 786440 | tf_op jit(solution)/shard_map/ppermute | solution.py:26
  85.2 3.6 %collective-permute-start.7 = (bf16[512,256]{0,1:T(8,128)(2,1)}, bf16[512,256]{0,1:T(8,128)(2,1)}, u32[]{:S(2)}, u32[]{:S(2)}) collective-permute-start(bf16[512,256]{0,1:T(8,128)(2,1)} %pad_maximum_fusion.2), channel_id=1, source_target_pairs={{0,1},{1,2},{2,3},{3,4},{4,5},{5,6},{6,7},{7,8},{8,9},{9,10},{10,1... | collective-permute-start | bytes 786440 | tf_op jit(solution)/shard_map/ppermute | solution.py:26
  88.9 2.6 fusion.29
  91.6 0.3 copy.32
  91.9 0.3 copy.33
  92.8 0.9 fusion.33
  93.8 1.3 fusion.41
  95.1 0.9 fusion.32
  96.1 2.7 collective-permute-done.7
  98.8 1.3 pad_maximum_fusion
  100.1 18.2 %while.14 = (s32[]{:T(128)}, f32[4,512]{1,0:T(4,128)S(1)}, f32[4,512]{1,0:T(4,128)S(1)}, f32[512,4,128]{0,2,1:T(8,128)S(1)}, s32[]{:T(128)}, /*index=5*/s32[2048...) while((s32[]{:T(128)}, f32[4,512]{1,0:T(4,128)S(1)}, ...), condition=%wide.region_8.9_spmd, body=%wide.region_5.8_spmd.sunk | while | flops 549197824 | bytes 33431808 | solution.py:89
  101.0 2.9 fusion.80
  104.0 3.8 %fusion.83 = f32[512,4,128]{0,2,1:T(8,128)S(1)} fusion(f32[512,512,4]{1,0,2:T(8,128)} %get-tuple-element.168, f32[4,512]{1,0:T(4,128)S(1)} %get-tuple-element.201, pred[512,512]{0,1:T(8,128)(4,1)S(1)} %broadcast_compare_fusion.3, f32[512,4,128]{0,2,1:T(8,128)S(1)} %get-tuple-element.188, f32[512,4]{0,1:T(4,128)S(1)} %get-tuple-element.169, ...), kind=kOutput, calls=%fused_computation.8.clone.1 | convolution fusion | flops 273154048 | bytes 6701064 | tf_op jit(solution)/shard_map/while/body/hqk,kd->qhd/dot_general | solution.py:56
  107.8 0.9 fusion.82
  109.7 2.9 fusion.80
  112.7 3.8 %fusion.83 = f32[512,4,128]{0,2,1:T(8,128)S(1)} fusion(f32[512,512,4]{1,0,2:T(8,128)} %get-tuple-element.168, f32[4,512]{1,0:T(4,128)S(1)} %get-tuple-element.201, pred[512,512]{0,1:T(8,128)(4,1)S(1)} %broadcast_compare_fusion.3, f32[512,4,128]{0,2,1:T(8,128)S(1)} %get-tuple-element.188, f32[512,4]{0,1:T(4,128)S(1)} %get-tuple-element.169, ...), kind=kOutput, calls=%fused_computation.8.clone.1 | convolution fusion | flops 273154048 | bytes 6701064 | tf_op jit(solution)/shard_map/while/body/hqk,kd->qhd/dot_general | solution.py:56
  116.5 0.9 fusion.82
  118.4 22.2 %all-gather.7.cloned.1.call-done = bf16[512,4096]{0,1:T(8,128)(2,1)} async-done(((bf16[512,32]{0,1:T(8,128)(2,1)}), bf16[512,4096]{0,1:T(8,128)(2,1)}) %all-gather.7.cloned.1.call-update) | async-done | bytes 4194320 | tf_op jit(solution)/shard_map/all_gather | solution.py:126
  140.7 5.9 %fusion.20 = bf16[512,4096]{1,0:T(8,128)(2,1)S(1)} fusion(bf16[512,4096]{1,0:T(8,128)(2,1)} %param.12, bf16[512,512]{0,1:T(8,128)(2,1)S(1)} %bitcast.82, bf16[512,4096]{0,1:T(8,128)(2,1)} %all-gather.7.cloned.1.call-done), kind=kOutput, calls=%fused_computation.28 | convolution fusion | flops 2153775104 | bytes 13107200 | tf_op jit(solution)/shard_map/dot_general | solution.py:124
  146.5 2.0 copy-done.2
  148.6 0.9 fusion.21
  149.5 65.5 %all-gather.9.cloned.1.call-done = bf16[4096,2048]{1,0:T(8,128)(2,1)} async-done(((bf16[128,2048]{1,0:T(8,128)(2,1)}), bf16[4096,2048]{1,0:T(8,128)(2,1)}) %all-gather.9.cloned.1.call-update) | async-done | bytes 16777232 | tf_op jit(solution)/shard_map/all_gather | solution.py:19
  214.9 8.4 %fusion.27 = f32[512,1024]{1,0:T(8,128)S(1)} fusion(bf16[4096,2048]{1,0:T(8,128)(2,1)} %all-gather.9.cloned.1.call-done, bf16[512,4096]{1,0:T(8,128)(2,1)} %copy-done.2, f32[4096]{0:T(1024)S(1)} %copy-done.9, f32[512]{0:T(512)S(1)} %add_rsqrt_fusion), kind=kOutput, calls=%fused_computation.35 | convolution fusion | flops 4303355904 | bytes 14698496 | tf_op jit(solution)/shard_map/dot_general | solution.py:135
  223.3 2.3 copy-done.6
  225.7 4.7 %multiply_convert_fusion = bf16[512,1024]{1,0:T(8,128)(2,1)S(1)} fusion(f32[512,1024]{1,0:T(8,128)S(1)} %fusion.27, bf16[4096,2048]{1,0:T(8,128)(2,1)S(1)} %copy-done.6, bf16[512,4096]{1,0:T(8,128)(2,1)S(1)} %copy-done.3, f32[4096]{0:T(1024)S(1)} %copy-done.9, f32[512]{0:T(512)S(1)} %add_rsqrt_fusion), kind=kOutput, calls=%fused_computation.46 | convolution fusion | flops 4306501632 | bytes 15747072 | tf_op jit(solution)/shard_map/dot_general | solution.py:136
  230.4 54.8 %all-gather.11.cloned.1.call-done = bf16[1024,4096]{0,1:T(8,128)(2,1)} async-done(((bf16[1024,32]{0,1:T(8,128)(2,1)}), bf16[1024,4096]{0,1:T(8,128)(2,1)}) %all-gather.11.cloned.1.call-update) | async-done | bytes 8388624 | tf_op jit(solution)/shard_map/all_gather | solution.py:140
  285.2 10.2 %fusion.24 = bf16[512,4096]{1,0:T(8,128)(2,1)} fusion(bf16[512,4096]{1,0:T(8,128)(2,1)} %copy-done.2, bf16[512,1024]{1,0:T(8,128)(2,1)S(1)} %multiply_convert_fusion, bf16[1024,4096]{0,1:T(8,128)(2,1)} %all-gather.11.cloned.1.call-done), kind=kOutput, calls=%fused_computation.32 | convolution fusion | flops 4301258752 | bytes 17825792 | tf_op jit(solution)/shard_map/dot_general | solution.py:138
  (63 shorter events, 2.1 us)
Async XLA Ops:
  6.5 62.9 %copy-start.8 = (f32[4096]{0:T(1024)S(1)}, f32[4096]{0:T(1024)}, u32[]{:S(2)}) copy-start(f32[4096]{0:T(1024)} %param.14) | copy-start | bytes 49156
  6.5 62.9 %all-gather.5.cloned.1.call-start = ((), (), s32[]{:S(2)}) async-start(), calls=%async_computation | async-start | bytes 6488064 | tf_op jit(solution)/shard_map/all_gather | solution.py:19
  20.4 120.3 %all-gather.7.cloned.1.call-start = ((), (), s32[]{:S(2)}) async-start(), calls=%async_computation.1 | async-start | bytes 4227072 | tf_op jit(solution)/shard_map/all_gather | solution.py:126
  21.2 193.8 %all-gather.9.cloned.1.call-start = ((), (), s32[]{:S(2)}) async-start(), calls=%async_computation.2 | async-start | bytes 17301504 | tf_op jit(solution)/shard_map/all_gather | solution.py:19
  35.6 249.6 %all-gather.11.cloned.1.call-start = ((), (), s32[]{:S(2)}) async-start(), calls=%async_computation.3 | async-start | bytes 8454144 | tf_op jit(solution)/shard_map/all_gather | solution.py:140
  36.4 16.9 %collective-permute-start = (s32[512]{0:T(512)S(1)}, s32[512]{0:T(512)S(1)}, u32[]{:S(2)}, u32[]{:S(2)}) collective-permute-start(s32[512]{0:T(512)S(1)} %broadcast_add_fusion), channel_id=1, source_target_pairs={{0,4},{1,5},{2,6},{3,7},{4,8},{5,9},{6,10},{7,11},{8,12},{9,13},{1... | collective-permute-start | bytes 6152 | tf_op jit(solution)/shard_map/ppermute | solution.py:26
  38.3 15.0 %collective-permute-start.1 = (s32[512]{0:T(512)S(1)}, s32[512]{0:T(512)S(1)}, u32[]{:S(2)}, u32[]{:S(2)}) collective-permute-start(s32[512]{0:T(512)S(1)} %broadcast_add_fusion), channel_id=1, source_target_pairs={{0,3},{1,4},{2,5},{3,6},{4,7},{5,8},{6,9},{7,10},{8,11},{9,12},{10... | collective-permute-start | bytes 6152 | tf_op jit(solution)/shard_map/ppermute | solution.py:26
  41.1 12.2 %collective-permute-start.2 = (s32[512]{0:T(512)S(1)}, s32[512]{0:T(512)S(1)}, u32[]{:S(2)}, u32[]{:S(2)}) collective-permute-start(s32[512]{0:T(512)S(1)} %broadcast_add_fusion), channel_id=1, source_target_pairs={{0,2},{1,3},{2,4},{3,5},{4,6},{5,7},{6,8},{7,9},{8,10},{9,11},{10,... | collective-permute-start | bytes 6152 | tf_op jit(solution)/shard_map/ppermute | solution.py:26
  44.2 9.1 %collective-permute-start.3 = (s32[512]{0:T(512)S(1)}, s32[512]{0:T(512)S(1)}, u32[]{:S(2)}, u32[]{:S(2)}) collective-permute-start(s32[512]{0:T(512)S(1)} %broadcast_add_fusion), channel_id=1, source_target_pairs={{0,1},{1,2},{2,3},{3,4},{4,5},{5,6},{6,7},{7,8},{8,9},{9,10},{10,1... | collective-permute-start | bytes 6152 | tf_op jit(solution)/shard_map/ppermute | solution.py:26
  69.4 19.4 %copy-start.1 = (bf16[512,4096]{1,0:T(8,128)(2,1)S(1)}, bf16[512,4096]{1,0:T(8,128)(2,1)}, u32[]{:S(2)}) copy-start(bf16[512,4096]{1,0:T(8,128)(2,1)} %param.12) | copy-start | bytes 12582916
  69.4 19.4 %copy-start.7 = (bf16[4096,768]{1,0:T(8,128)(2,1)S(1)}, bf16[4096,768]{1,0:T(8,128)(2,1)}, u32[]{:S(2)}) copy-start(bf16[4096,768]{1,0:T(8,128)(2,1)} %all-gather.5.cloned.1.call-done) | copy-start | bytes 18874372
  74.0 11.2 %copy-start.4 = (f32[512,256]{0,1:T(8,128)}, f32[512,256]{0,1:T(8,128)S(1)}, u32[]{:S(2)}) copy-start(f32[512,256]{0,1:T(8,128)S(1)} %fusion.34) | copy-start | bytes 1572868
  75.4 20.7 %collective-permute-start.4 = (bf16[512,256]{0,1:T(8,128)(2,1)}, bf16[512,256]{0,1:T(8,128)(2,1)}, u32[]{:S(2)}, u32[]{:S(2)}) collective-permute-start(bf16[512,256]{0,1:T(8,128)(2,1)} %pad_maximum_fusion.2), channel_id=1, source_target_pairs={{0,4},{1,5},{2,6},{3,7},{4,8},{5,9},{6,10},{7,11},{8,12},{9,13},{1... | collective-permute-start | bytes 786440 | tf_op jit(solution)/shard_map/ppermute | solution.py:26
  77.5 18.6 %collective-permute-start.5 = (bf16[512,256]{0,1:T(8,128)(2,1)}, bf16[512,256]{0,1:T(8,128)(2,1)}, u32[]{:S(2)}, u32[]{:S(2)}) collective-permute-start(bf16[512,256]{0,1:T(8,128)(2,1)} %pad_maximum_fusion.2), channel_id=1, source_target_pairs={{0,3},{1,4},{2,5},{3,6},{4,7},{5,8},{6,9},{7,10},{8,11},{9,12},{10... | collective-permute-start | bytes 786440 | tf_op jit(solution)/shard_map/ppermute | solution.py:26
  80.9 15.1 %collective-permute-start.6 = (bf16[512,256]{0,1:T(8,128)(2,1)}, bf16[512,256]{0,1:T(8,128)(2,1)}, u32[]{:S(2)}, u32[]{:S(2)}) collective-permute-start(bf16[512,256]{0,1:T(8,128)(2,1)} %pad_maximum_fusion.2), channel_id=1, source_target_pairs={{0,2},{1,3},{2,4},{3,5},{4,6},{5,7},{6,8},{7,9},{8,10},{9,11},{10,... | collective-permute-start | bytes 786440 | tf_op jit(solution)/shard_map/ppermute | solution.py:26
  85.2 13.6 %collective-permute-start.7 = (bf16[512,256]{0,1:T(8,128)(2,1)}, bf16[512,256]{0,1:T(8,128)(2,1)}, u32[]{:S(2)}, u32[]{:S(2)}) collective-permute-start(bf16[512,256]{0,1:T(8,128)(2,1)} %pad_maximum_fusion.2), channel_id=1, source_target_pairs={{0,1},{1,2},{2,3},{3,4},{4,5},{5,6},{6,7},{7,8},{8,9},{9,10},{10,1... | collective-permute-start | bytes 786440 | tf_op jit(solution)/shard_map/ppermute | solution.py:26
  92.5 1.3 copy-start.5
  104.0 3.8 %copy-start = (f32[512,512,4]{1,0,2:T(8,128)S(1)}, f32[512,512,4]{1,0,2:T(8,128)}, u32[]{:S(2)}) copy-start(f32[512,512,4]{1,0,2:T(8,128)} %get-tuple-element.168) | copy-start | bytes 12582916 | tf_op jit(solution)/shard_map/while
  112.7 3.8 %copy-start = (f32[512,512,4]{1,0,2:T(8,128)S(1)}, f32[512,512,4]{1,0,2:T(8,128)}, u32[]{:S(2)}) copy-start(f32[512,512,4]{1,0,2:T(8,128)} %get-tuple-element.168) | copy-start | bytes 12582916 | tf_op jit(solution)/shard_map/while
  146.5 2.0 copy-start.2
  148.6 66.4 %copy-start.9 = (f32[4096]{0:T(1024)S(1)}, f32[4096]{0:T(1024)}, u32[]{:S(2)}) copy-start(f32[4096]{0:T(1024)} %param.15) | copy-start | bytes 49156
  214.9 8.4 %copy-start.3 = (bf16[512,4096]{1,0:T(8,128)(2,1)S(1)}, bf16[512,4096]{1,0:T(8,128)(2,1)}, u32[]{:S(2)}) copy-start(bf16[512,4096]{1,0:T(8,128)(2,1)} %copy-done.2) | copy-start | bytes 12582916
  214.9 10.7 %copy-start.6 = (bf16[4096,2048]{1,0:T(8,128)(2,1)S(1)}, bf16[4096,2048]{1,0:T(8,128)(2,1)}, u32[]{:S(2)}) copy-start(bf16[4096,2048]{1,0:T(8,128)(2,1)} %all-gather.9.cloned.1.call-done) | copy-start | bytes 50331652
Sparse Core Ops, SparseCore 0:
  20.5 48.8 all-gather.4
  72.6 68.0 all-gather.6
  142.9 71.9 all-gather.8
  217.9 67.2 all-gather.10
where the time goes:
time: 307 us; the launch traced here: 302 us
  waiting for transfers between devices  161 us (52%)
  matrix products  52.1 us (17%)
  blocking collectives  26.6 us (9%)
  starting transfers between devices  25.5 us (8%)
  other arithmetic  15.6 us (5%)
  between operations  13.5 us (4%)
  local copies, waits for them, and re-layouts  5.88 us (2%)
    all_gather x2, waiting for transfers between devices, sent_together(): out = lax.all_gather(both, axis, axis=dim, tiled=True)  80.1 us
    all_gather x1, waiting for transfers between devices, per_device(): lax.all_gather(w_down, ('dp', 'fsdp'), axis=1, tiled=True)  54.8 us
    all_gather x2, blocking collectives, sent_together(): out = lax.all_gather(both, axis, axis=dim, tiled=True)  26.6 us
    ppermute x8, starting transfers between devices, shifted(): return lax.ppermute(array, axis, pairs)  25.4 us
    all_gather x1, waiting for transfers between devices, per_device(): lax.all_gather(w_out, ('dp', 'fsdp'), axis=1, tiled=True)  22.2 us
    dot_general x1, matrix products, per_device(): jnp.dot(hidden, lax.all_gather(w_down, ('dp', 'fsdp'), axis=1, tiled=True...  10.2 us
    dot_general x3, matrix products, weigh_values(): jnp.einsum('hqk,kd->qhd', weights.astype(jnp.bfloat16), values, preferred...  8.98 us
    dot_general x1, matrix products, per_device(): gate = jnp.dot(columns, pieces[0], preferred_element_type=jnp.float32)  8.4 us
  transfers between devices with their start and end apart: 12, of which 5 were waited for; matrix products, arithmetic and copies ran while one was open for 19% of the time, Pallas kernels for 0%

commit v1 on v0

--- a/solution.py
+++ b/solution.py
@@ -3,6 +3,7 @@
 import jax
 import jax.numpy as jnp
 from jax import lax
+from jax.sharding import Mesh
 from jax.sharding import PartitionSpec as P
 
 SPAN = 4
@@ -11,13 +12,8 @@
 EPS = 1e-05
 THETA = 500000.0
 NEGATIVE = -1e30
-
-
-def sent_together(arrays, axis, dim, along):
-    widths = [a.shape[along] for a in arrays]
-    both = jnp.concatenate(arrays, axis=along)
-    out = lax.all_gather(both, axis, axis=dim, tiled=True)
-    return tuple(jnp.split(out, [sum(widths[:k]) for k in range(1, len(widths))], axis=along))
+RANKS = ("y", "z", "core", "x")
+CHIPS = ("y", "z", "x")
 
 
 def shifted(array, axis, by):
@@ -90,73 +86,89 @@
     return mixed / jnp.transpose(totals)[:, :, None]
 
 
+def projection_weights(w_query, w_key_value):
+    both = jnp.concatenate([w_query, w_key_value], axis=1)
+    rows, width = both.shape
+    chips = lax.axis_size(CHIPS)
+    copies = lax.optimization_barrier(jnp.broadcast_to(both[None], (chips, rows, width)))
+    own = lax.all_to_all(copies, CHIPS, 0, 0, tiled=True)
+    other = lax.ppermute(own, "core", [(0, 1), (1, 0)])
+    inner = lax.axis_size("x") * rows
+    own = own.reshape(-1, 1, inner, width)
+    other = other.reshape(-1, 1, inner, width)
+    first = lax.axis_index("core") == 0
+    return jnp.concatenate(
+        [jnp.where(first, own, other), jnp.where(first, other, own)], axis=1
+    ).reshape(-1, width)
+
+
 def per_device(
     tokens, doc_ids, attn_gain, mlp_gain, w_query, w_key_value, w_out, w_gate, w_up, w_down
 ):
     rows = tokens.shape[0]
-    rank = lax.axis_index(("dp", "fsdp"))
+    rank = lax.axis_index(RANKS)
+    hidden_width = w_gate.shape[1]
+    rest = jnp.concatenate([w_gate, w_up, w_out.T, w_down.T], axis=1)
+    rest = lax.all_gather(rest, RANKS, axis=0, tiled=True)
+
     normed = rms_scale(tokens, attn_gain)
     query_width = w_query.shape[1]
     pair_width = w_key_value.shape[1]
     head = pair_width // 2
     heads = query_width // head
-    group_query, group_pair = sent_together((w_query, w_key_value), "fsdp", 0, 1)
-    pieces = sent_together((group_query, group_pair), "dp", 0, 1)
-    columns = normed
-    query_raw = jnp.dot(columns, pieces[0], preferred_element_type=jnp.float32)
-    pair_raw = jnp.dot(columns, pieces[1], preferred_element_type=jnp.float32)
+    w_project = projection_weights(w_query, w_key_value)
+    raw = jnp.dot(normed, w_project, preferred_element_type=jnp.float32)
+    query_raw = raw[:, :query_width]
+    pair_raw = raw[:, query_width:]
     position = rank * rows + jnp.arange(rows, dtype=jnp.int32)
     query = rotate(query_raw.reshape(rows, heads, head), position).astype(jnp.bfloat16)
     keys = rotate(pair_raw[:, None, :head], position)[:, 0, :].astype(jnp.bfloat16)
     values = pair_raw[:, head:].astype(jnp.bfloat16)
     own_pairs = jnp.concatenate([keys, values], axis=1)
     marks = doc_ids + 1
+    mark_rows = marks.astype(jnp.bfloat16).reshape(-1, pair_width)
+    sent = jnp.concatenate([own_pairs, mark_rows], axis=0)
     pair_pieces = []
     mark_pieces = []
     for distance in range(SPAN, 0, -1):
-        moved_pairs, moved_marks = shifted((own_pairs, marks), ("dp", "fsdp"), distance)
-        pair_pieces.append(moved_pairs)
-        mark_pieces.append(moved_marks)
+        moved = shifted(sent, RANKS, distance)
+        pair_pieces.append(moved[:rows])
+        mark_pieces.append(moved[rows:].reshape(-1).astype(jnp.int32))
     halo_pairs = jnp.concatenate(pair_pieces, axis=0)
     halo_marks = jnp.concatenate(mark_pieces, axis=0)
     mixed = attend_live(query, halo_pairs, halo_marks, own_pairs, marks, rows)
     attended = mixed.reshape(rows, query_width).astype(jnp.bfloat16)
-    projected = jnp.dot(
-        attended,
-        lax.all_gather(w_out, ("dp", "fsdp"), axis=1, tiled=True),
-        preferred_element_type=jnp.float32,
+    g, u, o = hidden_width, 2 * hidden_width, 2 * hidden_width + query_width
+    projected = lax.dot_general(
+        attended, rest[:, u:o], (((1,), (1,)), ((), ())), preferred_element_type=jnp.float32
     )
     resid = (tokens.astype(jnp.float32) + projected).astype(jnp.bfloat16)
     resid = lax.optimization_barrier(resid)
     normed_mlp = rms_scale(resid, mlp_gain)
-    group_gate, group_up = sent_together((w_gate, w_up), "fsdp", 0, 1)
-    pieces = sent_together((group_gate, group_up), "dp", 0, 1)
-    columns = normed_mlp
-    gate = jnp.dot(columns, pieces[0], preferred_element_type=jnp.float32)
-    up_value = jnp.dot(columns, pieces[1], preferred_element_type=jnp.float32)
+    gate = jnp.dot(normed_mlp, rest[:, :g], preferred_element_type=jnp.float32)
+    up_value = jnp.dot(normed_mlp, rest[:, g:u], preferred_element_type=jnp.float32)
     hidden = (jax.nn.silu(gate) * up_value).astype(jnp.bfloat16)
-    down = jnp.dot(
-        hidden,
-        lax.all_gather(w_down, ("dp", "fsdp"), axis=1, tiled=True),
-        preferred_element_type=jnp.float32,
+    down = lax.dot_general(
+        hidden, rest[:, o:], (((1,), (1,)), ((), ())), preferred_element_type=jnp.float32
     )
     return (resid.astype(jnp.float32) + down).astype(jnp.bfloat16)
 
 
 def solution(mesh):
+    chips = Mesh(mesh.devices.reshape(4, 4, 2, 4), RANKS)
     in_specs = (
-        P(("dp", "fsdp"), None),
-        P(("dp", "fsdp")),
+        P(RANKS, None),
+        P(RANKS),
         P(),
         P(),
-        P(("dp", "fsdp"), None),
-        P(("dp", "fsdp"), None),
-        P(None, ("dp", "fsdp")),
-        P(("dp", "fsdp"), None),
-        P(("dp", "fsdp"), None),
-        P(None, ("dp", "fsdp")),
+        P(RANKS, None),
+        P(RANKS, None),
+        P(None, RANKS),
+        P(RANKS, None),
+        P(RANKS, None),
+        P(None, RANKS),
     )
-    out_specs = P(("dp", "fsdp"), None)
+    out_specs = P(RANKS, None)
     return jax.shard_map(
-        per_device, mesh=mesh, in_specs=in_specs, out_specs=out_specs, check_vma=False
+        per_device, mesh=chips, in_specs=in_specs, out_specs=out_specs, check_vma=False
     )

time: 307 us -> 200 us (0.65); the launches traced: 302 us -> 199 us
  waiting for transfers between devices: 161 us -> 18.9 us
  blocking collectives: 26.6 us -> 50.3 us
  starting transfers between devices: 25.5 us -> 13.3 us
  matrix products: 52.1 us -> 63.7 us
  local copies, waits for them, and re-layouts: 5.88 us -> 14.2 us
  other arithmetic: 15.6 us -> 21.5 us
    all_gather x4 -> x1, waiting for transfers between devices: 157 us -> 0.02 us  [per_device(): rest = lax.all_gather(rest, RANKS, axis=0, tiled=True)]
    all_to_all x0 -> x1, blocking collectives: none -> 50.3 us  [projection_weights(): own = lax.all_to_all(copies, CHIPS, 0, 0, tiled=True)]
    all_gather x2 -> x0, blocking collectives: 26.6 us -> none  [sent_together(): out = lax.all_gather(both, axis, axis=dim, tiled=True)]
    ppermute x8 -> x4, waiting for transfers between devices: 2.71 us -> 18.8 us  [shifted(): return lax.ppermute(array, axis, pairs)]
    ppermute x8 -> x4, starting transfers between devices: 25.4 us -> 13.3 us  [shifted(): return lax.ppermute(array, axis, pairs)]
    slice x1 -> x15, local copies, waits for them, and re-layouts: 0.1 us -> 9.87 us  [the longest x4 3.89 us: per_device(): pair_pieces.append(moved[:rows])]
    dot_general x3 -> x5, matrix products: 8.98 us -> 17.1 us  [weigh_values(): jnp.einsum('hqk,kd->qhd', weights.astype(jnp.bfloat16), values, preferred...]
    dot_general x3 -> x5, matrix products: 6.81 us -> 12.7 us  [head_scores(): jnp.einsum('qhd,kd->hqk', query, keys, preferred_element_type=jnp.float32)]
  transfers between devices with their start and end apart: 12 -> 6, of which waited for: 5 -> 2; matrix products, arithmetic and copies ran while one was open for 19% -> 33% of each run, Pallas kernels for 0% -> 0%
where the time goes in v1:
time: 200 us; the launch traced here: 199 us
  matrix products  63.7 us (32%)
  blocking collectives  50.3 us (25%)
  other arithmetic  21.5 us (11%)
  waiting for transfers between devices  18.9 us (9%)
  local copies, waits for them, and re-layouts  14.2 us (7%)
  between operations  13.7 us (7%)
  starting transfers between devices  13.3 us (7%)
  loops' own time  3.2 us (2%)
    all_to_all x1, blocking collectives, projection_weights(): own = lax.all_to_all(copies, CHIPS, 0, 0, tiled=True)  50.3 us
    ppermute x4, waiting for transfers between devices, shifted(): return lax.ppermute(array, axis, pairs)  18.8 us
    dot_general x5, matrix products, weigh_values(): jnp.einsum('hqk,kd->qhd', weights.astype(jnp.bfloat16), values, preferred...  17.1 us
    ppermute x4, starting transfers between devices, shifted(): return lax.ppermute(array, axis, pairs)  13.3 us
    dot_general x5, matrix products, head_scores(): jnp.einsum('qhd,kd->hqk', query, keys, preferred_element_type=jnp.float32)  12.7 us
    dot_general x1, matrix products, per_device(): lax.dot_general(hidden, rest[:, o:], (((1,), (1,)), ((), ())), preferred_...  9.49 us
    dot_general x1, matrix products, per_device(): jnp.dot(normed_mlp, rest[:, g:u], preferred_element_type=jnp.float32)  8.09 us
    dot_general x1, matrix products, per_device(): gate = jnp.dot(normed_mlp, rest[:, :g], preferred_element_type=jnp.float32)  6.97 us
  transfers between devices with their start and end apart: 6, of which 2 were waited for; matrix products, arithmetic and copies ran while one was open for 33% of the time, Pallas kernels for 0%

profile of v1, /device:TPU:98, one launch (start us, length us, event | category | flops | bytes accessed | tf_op | source)
XLA Modules:
  0.0 198.8 jit_solution(15487745132083716691)
XLA Ops:
  6.5 1.6 pad_maximum_fusion.4
  8.2 0.8 pad_maximum_fusion.7
  9.4 50.3 %all_to_all.5 = bf16[64,32,768]{2,1,0:T(8,128)(2,1)S(1)} all-to-all(bf16[64,32,768]{2,1,0:T(8,128)(2,1)S(1)} %broadcast_in_dim.25), channel_id=1, replica_groups=mesh['y'=4,'z'=4,'core'=2,'x'=4] {'y','z','x'}, dimensions={0} | all-to-all | bytes 6291456 | tf_op jit(solution)/shard_map/all_to_all | solution.py:94
  59.7 0.8 copy.46
  61.0 3.1 %fusion.17 = f32[512]{0:T(512)S(1)} fusion(bf16[512,4096]{1,0:T(8,128)(2,1)} %param.12), kind=kLoop, calls=%fused_computation.25 | loop fusion | flops 6290944 | bytes 4196352 | tf_op jit(solution)/shard_map/reduce_sum | solution.py:27
  64.3 1.8 multiply_cosine_fusion
  66.1 2.6 %broadcast_select_fusion.1 = (bf16[64,32,768]{2,1,0:T(8,128)(2,1)S(1)}, bf16[64,32,768]{2,1,0:T(8,128)(2,1)S(1)}) fusion(bf16[64,32,768]{2,1,0:T(8,128)(2,1)S(1)} %all_to_all.5, bf16[64,32,768]{2,1,0:T(8,128)(2,1)} %collective-permute-done, pred[]{:T(512)S(6)} %eq.49), kind=kLoop, calls=%fused_computation.50 | loop fusion | flops 3145728 | bytes 12582913 | tf_op jit(solution)/shard_map/jit(_where)/select_n | solution.py:101
  69.3 1.6 copy-done.1
  70.9 3.5 %fusion.33 = f32[512,768]{1,0:T(8,128)S(1)} fusion(bf16[4096,768]{1,0:T(8,128)(2,1)S(1)} %bitcast.93, bf16[512,4096]{1,0:T(8,128)(2,1)S(1)} %copy-done.1, f32[4096]{0:T(1024)S(1)} %copy-done.6, f32[512]{0:T(512)S(1)} %add_rsqrt_fusion.1), kind=kOutput, calls=%fused_computation.40 | convolution fusion | flops 3229614080 | bytes 12077056 | tf_op jit(solution)/shard_map/dot_general | solution.py:120
  75.3 1.6 pad_maximum_fusion.3
  77.0 2.3 %collective-permute-start.1 = (bf16[514,256]{0,1:T(8,128)(2,1)}, bf16[514,256]{0,1:T(8,128)(2,1)}, u32[]{:S(2)}, u32[]{:S(2)}) collective-permute-start(bf16[514,256]{0,1:T(8,128)(2,1)} %pad_maximum_fusion.3), channel_id=1, source_target_pairs={{0,4},{1,5},{2,6},{3,7},{4,8},{5,9},{6,10},{7,11},{8,12},{9,13},{1... | collective-permute-start | bytes 789512 | tf_op jit(solution)/shard_map/ppermute | solution.py:22
  79.3 5.5 %collective-permute-start.2 = (bf16[514,256]{0,1:T(8,128)(2,1)}, bf16[514,256]{0,1:T(8,128)(2,1)}, u32[]{:S(2)}, u32[]{:S(2)}) collective-permute-start(bf16[514,256]{0,1:T(8,128)(2,1)} %pad_maximum_fusion.3), channel_id=1, source_target_pairs={{0,3},{1,4},{2,5},{3,6},{4,7},{5,8},{6,9},{7,10},{8,11},{9,12},{10... | collective-permute-start | bytes 789512 | tf_op jit(solution)/shard_map/ppermute | solution.py:22
  84.8 2.7 %collective-permute-start.3 = (bf16[514,256]{0,1:T(8,128)(2,1)}, bf16[514,256]{0,1:T(8,128)(2,1)}, u32[]{:S(2)}, u32[]{:S(2)}) collective-permute-start(bf16[514,256]{0,1:T(8,128)(2,1)} %pad_maximum_fusion.3), channel_id=1, source_target_pairs={{0,2},{1,3},{2,4},{3,5},{4,6},{5,7},{6,8},{7,9},{8,10},{9,11},{10,... | collective-permute-start | bytes 789512 | tf_op jit(solution)/shard_map/ppermute | solution.py:22
  87.6 2.7 %collective-permute-start.4 = (bf16[514,256]{0,1:T(8,128)(2,1)}, bf16[514,256]{0,1:T(8,128)(2,1)}, u32[]{:S(2)}, u32[]{:S(2)}) collective-permute-start(bf16[514,256]{0,1:T(8,128)(2,1)} %pad_maximum_fusion.3), channel_id=1, source_target_pairs={{0,1},{1,2},{2,3},{3,4},{4,5},{5,6},{6,7},{7,8},{8,9},{9,10},{10,1... | collective-permute-start | bytes 789512 | tf_op jit(solution)/shard_map/ppermute | solution.py:22
  90.3 1.6 slice.93
  92.3 0.6 fusion.68
  93.5 0.9 fusion.40
  94.4 0.9 fusion.39
  95.4 1.4 fusion.46
  96.7 0.8 slice.97
  97.7 0.9 slice.98
  98.6 11.7 %collective-permute-done.3 = bf16[514,256]{0,1:T(8,128)(2,1)} collective-permute-done((bf16[514,256]{0,1:T(8,128)(2,1)}, bf16[514,256]{0,1:T(8,128)(2,1)}, u32[]{:S(2)}, u32[]{:S(2)}) %collective-permute-start.3) | collective-permute-done | bytes 263200 | tf_op jit(solution)/shard_map/ppermute | solution.py:22
  110.3 0.8 slice.99
  111.2 7.2 %collective-permute-done.4 = bf16[514,256]{0,1:T(8,128)(2,1)} collective-permute-done((bf16[514,256]{0,1:T(8,128)(2,1)}, bf16[514,256]{0,1:T(8,128)(2,1)}, u32[]{:S(2)}, u32[]{:S(2)}) %collective-permute-start.4) | collective-permute-done | bytes 263200 | tf_op jit(solution)/shard_map/ppermute | solution.py:22
  118.4 0.9 slice.100
  119.3 0.6 broadcast_compare_fusion.1
  120.1 1.0 slice.101
  121.1 1.0 slice.102
  122.1 1.0 slice.103
  123.1 1.0 slice.104
  124.8 35.7 %while.14 = (s32[]{:T(128)}, f32[4,512]{1,0:T(4,128)S(1)}, f32[4,512]{1,0:T(4,128)S(1)}, f32[512,4,128]{0,2,1:T(8,128)S(1)}, s32[]{:T(128)}, /*index=5*/s32[2048...) while((s32[]{:T(128)}, f32[4,512]{1,0:T(4,128)S(1)}, ...), condition=%wide.region_8.9_spmd, body=%wide.region_5.8_spmd.sunk | while | flops 549197824 | bytes 33431808 | solution.py:85
  125.6 2.9 %fusion.82 = (f32[4,512]{1,0:T(4,128)S(1)}, f32[512,512,4]{1,0,2:T(8,128)}) fusion(pred[512,512]{0,1:T(8,128)(4,1)S(1)} %broadcast_compare_fusion.3, bf16[512,4,128]{2,0,1:T(8,128)(2,1)S(1)} %get-tuple-element.212, bf16[2048,256]{0,1:T(8,128)(2,1)S(1)} %get-tuple-element.211, s32[]{:T(128)S(6)} %select_n.85), kind=kOutput, calls=%fused_computation.4.clone.1 | convolution fusion | flops 271579136 | bytes 5120004 | tf_op jit(solution)/shard_map/while/body/qhd,kd->hqk/dot_general | solution.py:46
  128.6 4.0 %fusion.85 = f32[512,4,128]{0,2,1:T(8,128)S(1)} fusion(f32[512,512,4]{1,0,2:T(8,128)} %get-tuple-element.172, f32[4,512]{1,0:T(4,128)S(1)} %get-tuple-element.205, pred[512,512]{0,1:T(8,128)(4,1)S(1)} %broadcast_compare_fusion.3, f32[512,4,128]{0,2,1:T(8,128)S(1)} %get-tuple-element.192, f32[512,4]{0,1:T(4,128)S(1)} %get-tuple-element.173, ...), kind=kOutput, calls=%fused_computation.8.clone.1 | convolution fusion | flops 273154048 | bytes 6701064 | tf_op jit(solution)/shard_map/while/body/hqk,kd->qhd/dot_general | solution.py:52
  132.6 0.9 fusion.84
  134.4 2.9 %fusion.82 = (f32[4,512]{1,0:T(4,128)S(1)}, f32[512,512,4]{1,0,2:T(8,128)}) fusion(pred[512,512]{0,1:T(8,128)(4,1)S(1)} %broadcast_compare_fusion.3, bf16[512,4,128]{2,0,1:T(8,128)(2,1)S(1)} %get-tuple-element.212, bf16[2048,256]{0,1:T(8,128)(2,1)S(1)} %get-tuple-element.211, s32[]{:T(128)S(6)} %select_n.85), kind=kOutput, calls=%fused_computation.4.clone.1 | convolution fusion | flops 271579136 | bytes 5120004 | tf_op jit(solution)/shard_map/while/body/qhd,kd->hqk/dot_general | solution.py:46
  137.4 4.1 %fusion.85 = f32[512,4,128]{0,2,1:T(8,128)S(1)} fusion(f32[512,512,4]{1,0,2:T(8,128)} %get-tuple-element.172, f32[4,512]{1,0:T(4,128)S(1)} %get-tuple-element.205, pred[512,512]{0,1:T(8,128)(4,1)S(1)} %broadcast_compare_fusion.3, f32[512,4,128]{0,2,1:T(8,128)S(1)} %get-tuple-element.192, f32[512,4]{0,1:T(4,128)S(1)} %get-tuple-element.173, ...), kind=kOutput, calls=%fused_computation.8.clone.1 | convolution fusion | flops 273154048 | bytes 6701064 | tf_op jit(solution)/shard_map/while/body/hqk,kd->qhd/dot_general | solution.py:52
  141.5 0.9 fusion.84
  143.3 2.9 %fusion.82 = (f32[4,512]{1,0:T(4,128)S(1)}, f32[512,512,4]{1,0,2:T(8,128)}) fusion(pred[512,512]{0,1:T(8,128)(4,1)S(1)} %broadcast_compare_fusion.3, bf16[512,4,128]{2,0,1:T(8,128)(2,1)S(1)} %get-tuple-element.212, bf16[2048,256]{0,1:T(8,128)(2,1)S(1)} %get-tuple-element.211, s32[]{:T(128)S(6)} %select_n.85), kind=kOutput, calls=%fused_computation.4.clone.1 | convolution fusion | flops 271579136 | bytes 5120004 | tf_op jit(solution)/shard_map/while/body/qhd,kd->hqk/dot_general | solution.py:46
  146.3 3.8 %fusion.85 = f32[512,4,128]{0,2,1:T(8,128)S(1)} fusion(f32[512,512,4]{1,0,2:T(8,128)} %get-tuple-element.172, f32[4,512]{1,0:T(4,128)S(1)} %get-tuple-element.205, pred[512,512]{0,1:T(8,128)(4,1)S(1)} %broadcast_compare_fusion.3, f32[512,4,128]{0,2,1:T(8,128)S(1)} %get-tuple-element.192, f32[512,4]{0,1:T(4,128)S(1)} %get-tuple-element.173, ...), kind=kOutput, calls=%fused_computation.8.clone.1 | convolution fusion | flops 273154048 | bytes 6701064 | tf_op jit(solution)/shard_map/while/body/hqk,kd->qhd/dot_general | solution.py:52
  150.1 0.9 fusion.84
  151.9 2.9 %fusion.82 = (f32[4,512]{1,0:T(4,128)S(1)}, f32[512,512,4]{1,0,2:T(8,128)}) fusion(pred[512,512]{0,1:T(8,128)(4,1)S(1)} %broadcast_compare_fusion.3, bf16[512,4,128]{2,0,1:T(8,128)(2,1)S(1)} %get-tuple-element.212, bf16[2048,256]{0,1:T(8,128)(2,1)S(1)} %get-tuple-element.211, s32[]{:T(128)S(6)} %select_n.85), kind=kOutput, calls=%fused_computation.4.clone.1 | convolution fusion | flops 271579136 | bytes 5120004 | tf_op jit(solution)/shard_map/while/body/qhd,kd->hqk/dot_general | solution.py:46
  154.9 3.8 %fusion.85 = f32[512,4,128]{0,2,1:T(8,128)S(1)} fusion(f32[512,512,4]{1,0,2:T(8,128)} %get-tuple-element.172, f32[4,512]{1,0:T(4,128)S(1)} %get-tuple-element.205, pred[512,512]{0,1:T(8,128)(4,1)S(1)} %broadcast_compare_fusion.3, f32[512,4,128]{0,2,1:T(8,128)S(1)} %get-tuple-element.192, f32[512,4]{0,1:T(4,128)S(1)} %get-tuple-element.173, ...), kind=kOutput, calls=%fused_computation.8.clone.1 | convolution fusion | flops 273154048 | bytes 6701064 | tf_op jit(solution)/shard_map/while/body/hqk,kd->qhd/dot_general | solution.py:52
  158.7 0.9 fusion.84
  160.6 5.9 %fusion.20 = bf16[512,4096]{1,0:T(8,128)(2,1)S(1)} fusion(bf16[512,4096]{1,0:T(8,128)(2,1)} %param.12, bf16[512,512]{0,1:T(8,128)(2,1)S(1)} %bitcast.95, bf16[4096,3584]{1,0:T(8,128)(2,1)} %all-gather.2.cloned.1.call-done), kind=kOutput, calls=%fused_computation.28 | convolution fusion | flops 2153775104 | bytes 13107200 | tf_op jit(solution)/shard_map/dot_general | solution.py:142
  166.5 0.9 fusion.21
  167.4 7.0 %fusion.29 = f32[512,1024]{1,0:T(8,128)S(1)} fusion(bf16[4096,3584]{1,0:T(8,128)(2,1)} %all-gather.2.cloned.1.call-done, bf16[512,4096]{1,0:T(8,128)(2,1)S(1)} %fusion.20, f32[4096]{0:T(1024)S(1)} %copy-done.7, f32[512]{0:T(512)S(1)} %add_rsqrt_fusion), kind=kOutput, calls=%fused_computation.37 | convolution fusion | flops 4303355904 | bytes 14698496 | tf_op jit(solution)/shard_map/dot_general | solution.py:148
  174.4 8.1 %multiply_convert_fusion = bf16[512,1024]{1,0:T(8,128)(2,1)S(1)} fusion(f32[512,1024]{1,0:T(8,128)S(1)} %fusion.29, bf16[4096,3584]{1,0:T(8,128)(2,1)} %all-gather.2.cloned.1.call-done, bf16[512,4096]{1,0:T(8,128)(2,1)S(1)} %fusion.20, f32[4096]{0:T(1024)S(1)} %copy-done.7, f32[512]{0:T(512)S(1)} %add_rsqrt_fusion), kind=kOutput, calls=%fused_computation.51 | convolution fusion | flops 4306501632 | bytes 15747072 | tf_op jit(solution)/shard_map/dot_general | solution.py:149
  182.5 9.5 %fusion.24 = bf16[512,4096]{1,0:T(8,128)(2,1)} fusion(bf16[512,4096]{1,0:T(8,128)(2,1)S(1)} %fusion.20, bf16[512,1024]{1,0:T(8,128)(2,1)S(1)} %multiply_convert_fusion, bf16[4096,3584]{1,0:T(8,128)(2,1)} %all-gather.2.cloned.1.call-done), kind=kOutput, calls=%fused_computation.32 | convolution fusion | flops 4301258752 | bytes 17825792 | tf_op jit(solution)/shard_map/dot_general | solution.py:151
  (81 shorter events, 6.3 us)
Async XLA Ops:
  6.5 154.1 %all-gather.2.cloned.1.call-start = ((), (), s32[]{:S(2)}) async-start(), calls=%async_computation.1 | async-start | bytes 29589504 | tf_op jit(solution)/shard_map/all_gather | solution.py:112
  9.0 50.7 %copy-start.5 = (s32[512]{0:T(512)S(1)}, s32[512]{0:T(512)}, u32[]{:S(2)}) copy-start(s32[512]{0:T(512)} %param.13) | copy-start | bytes 6148
  59.7 6.5 %collective-permute-start = (bf16[64,32,768]{2,1,0:T(8,128)(2,1)S(1)}, bf16[64,32,768]{2,1,0:T(8,128)(2,1)}, u32[]{:S(2)}, u32[]{:S(2)}) collective-permute-start(bf16[64,32,768]{2,1,0:T(8,128)(2,1)S(1)} %all_to_all.5), channel_id=1, source_target_pairs={{0,4},{4,0},{1,5},{5,1},{2,6},{6,2},{3,7},{7,3},{8,12},{12,8},{9,1... | collective-permute-start | bytes 9437192 | tf_op jit(solution)/shard_map/ppermute | solution.py:95
  68.7 2.2 %copy-start.1 = (bf16[512,4096]{1,0:T(8,128)(2,1)S(1)}, bf16[512,4096]{1,0:T(8,128)(2,1)}, u32[]{:S(2)}) copy-start(bf16[512,4096]{1,0:T(8,128)(2,1)} %param.12) | copy-start | bytes 12582916
  68.7 2.2 %copy-start.6 = (f32[4096]{0:T(1024)S(1)}, f32[4096]{0:T(1024)}, u32[]{:S(2)}) copy-start(f32[4096]{0:T(1024)} %param.14) | copy-start | bytes 49156
  74.4 13.1 %copy-start.2 = (f32[512,768]{1,0:T(8,128)}, f32[512,768]{1,0:T(8,128)S(1)}, u32[]{:S(2)}) copy-start(f32[512,768]{1,0:T(8,128)S(1)} %fusion.33) | copy-start | bytes 4718596
  77.0 15.9 %copy-start.3 = (f32[512,64]{1,0:T(8,128)S(1)}, f32[512,64]{1,0:T(8,128)}, u32[]{:S(2)}) copy-start(f32[512,64]{1,0:T(8,128)} %get-tuple-element.104) | copy-start | bytes 393220
  77.0 15.9 %copy-start.4 = (f32[512,64]{1,0:T(8,128)S(1)}, f32[512,64]{1,0:T(8,128)}, u32[]{:S(2)}) copy-start(f32[512,64]{1,0:T(8,128)} %get-tuple-element.105) | copy-start | bytes 393220
  77.0 19.8 %collective-permute-start.1 = (bf16[514,256]{0,1:T(8,128)(2,1)}, bf16[514,256]{0,1:T(8,128)(2,1)}, u32[]{:S(2)}, u32[]{:S(2)}) collective-permute-start(bf16[514,256]{0,1:T(8,128)(2,1)} %pad_maximum_fusion.3), channel_id=1, source_target_pairs={{0,4},{1,5},{2,6},{3,7},{4,8},{5,9},{6,10},{7,11},{8,12},{9,13},{1... | collective-permute-start | bytes 789512 | tf_op jit(solution)/shard_map/ppermute | solution.py:22
  79.3 18.4 %collective-permute-start.2 = (bf16[514,256]{0,1:T(8,128)(2,1)}, bf16[514,256]{0,1:T(8,128)(2,1)}, u32[]{:S(2)}, u32[]{:S(2)}) collective-permute-start(bf16[514,256]{0,1:T(8,128)(2,1)} %pad_maximum_fusion.3), channel_id=1, source_target_pairs={{0,3},{1,4},{2,5},{3,6},{4,7},{5,8},{6,9},{7,10},{8,11},{9,12},{10... | collective-permute-start | bytes 789512 | tf_op jit(solution)/shard_map/ppermute | solution.py:22
  84.8 25.5 %collective-permute-start.3 = (bf16[514,256]{0,1:T(8,128)(2,1)}, bf16[514,256]{0,1:T(8,128)(2,1)}, u32[]{:S(2)}, u32[]{:S(2)}) collective-permute-start(bf16[514,256]{0,1:T(8,128)(2,1)} %pad_maximum_fusion.3), channel_id=1, source_target_pairs={{0,2},{1,3},{2,4},{3,5},{4,6},{5,7},{6,8},{7,9},{8,10},{9,11},{10,... | collective-permute-start | bytes 789512 | tf_op jit(solution)/shard_map/ppermute | solution.py:22
  87.6 30.8 %collective-permute-start.4 = (bf16[514,256]{0,1:T(8,128)(2,1)}, bf16[514,256]{0,1:T(8,128)(2,1)}, u32[]{:S(2)}, u32[]{:S(2)}) collective-permute-start(bf16[514,256]{0,1:T(8,128)(2,1)} %pad_maximum_fusion.3), channel_id=1, source_target_pairs={{0,1},{1,2},{2,3},{3,4},{4,5},{5,6},{6,7},{7,8},{8,9},{9,10},{10,1... | collective-permute-start | bytes 789512 | tf_op jit(solution)/shard_map/ppermute | solution.py:22
  128.6 4.0 %copy-start = (f32[512,512,4]{1,0,2:T(8,128)S(1)}, f32[512,512,4]{1,0,2:T(8,128)}, u32[]{:S(2)}) copy-start(f32[512,512,4]{1,0,2:T(8,128)} %get-tuple-element.172) | copy-start | bytes 12582916 | tf_op jit(solution)/shard_map/while
  137.4 4.1 %copy-start = (f32[512,512,4]{1,0,2:T(8,128)S(1)}, f32[512,512,4]{1,0,2:T(8,128)}, u32[]{:S(2)}) copy-start(f32[512,512,4]{1,0,2:T(8,128)} %get-tuple-element.172) | copy-start | bytes 12582916 | tf_op jit(solution)/shard_map/while
  146.3 3.8 %copy-start = (f32[512,512,4]{1,0,2:T(8,128)S(1)}, f32[512,512,4]{1,0,2:T(8,128)}, u32[]{:S(2)}) copy-start(f32[512,512,4]{1,0,2:T(8,128)} %get-tuple-element.172) | copy-start | bytes 12582916 | tf_op jit(solution)/shard_map/while
  154.9 3.8 %copy-start = (f32[512,512,4]{1,0,2:T(8,128)S(1)}, f32[512,512,4]{1,0,2:T(8,128)}, u32[]{:S(2)}) copy-start(f32[512,512,4]{1,0,2:T(8,128)} %get-tuple-element.172) | copy-start | bytes 12582916 | tf_op jit(solution)/shard_map/while
  166.5 0.9 copy-start.7
Sparse Core Ops, SparseCore 0:
  10.3 135.8 all-gather.1
